TPU v7x, 32 devices: a whole 2x2x4 slice. The times are simulated.
32 devices in a mesh: data: 32 (over z, y, x, core).
Axes of the slice: x: 2, y: 2, z: 4, core: 2. Of those that a mesh axis runs over, the one named last changes fastest.
Arguments:
- tokens: bfloat16 [8192, 1280], P('data')
- labels: int32 [3, 8192], P(None, 'data')
- w_one: bfloat16 [1280, 5120], replicated
- w_two: bfloat16 [5120, 1280], replicated
- adapter_a: bfloat16 [1280, 8], replicated
- adapter_b: bfloat16 [8, 5120], replicated
- task_heads: bfloat16 [3, 1280, 13], replicated
Outputs:
- output 1: float32 [3], replicated
- output 2: float32 [1280, 8], P('data')
- output 3: float32 [8, 5120], P(None, 'data')
All inputs are finite; a program needn't handle non-finite values.
Results may differ from a plain program's by a relative error of at most 0.00237.
Values are sent between devices in bfloat16 or wider.
A program may use at most 1 GiB of HBM per device.

v0:
```python
import jax
import jax.numpy as jnp
from jax import lax
from jax.sharding import PartitionSpec as P

EG_STEPS = 20


def weight_solver(gram_mat):
    num_tasks = gram_mat.shape[0]
    eg_scale = jnp.trace(gram_mat) / num_tasks

    def eg_step(step_idx, weights):
        weights = weights * jnp.exp(-jnp.sum(gram_mat * weights[None, :], axis=1) / eg_scale)
        return weights / jnp.sum(weights)

    return lax.fori_loop(0, EG_STEPS, eg_step, jnp.full((num_tasks,), 1.0 / num_tasks, jnp.float32))


def task_grads(tokens, labels, w_one, w_two, adapter_a, adapter_b, task_heads):
    num_classes = task_heads.shape[2]
    low_rank = jnp.dot(tokens, adapter_a, preferred_element_type=jnp.float32).astype(jnp.bfloat16)
    pre_act = jnp.dot(tokens, w_one, preferred_element_type=jnp.float32) + jnp.dot(low_rank, adapter_b, preferred_element_type=jnp.float32)
    gelu_out, gelu_slope = jax.jvp(jax.nn.gelu, (pre_act,), (jnp.ones_like(pre_act),))
    hidden = gelu_out.astype(jnp.bfloat16)
    trunk_out = (tokens.astype(jnp.float32) + jnp.dot(hidden, w_two, preferred_element_type=jnp.float32)).astype(jnp.bfloat16)
    logits = jnp.einsum("bd,tdc->tbc", trunk_out, task_heads, preferred_element_type=jnp.float32)
    task_probs = jax.nn.softmax(logits, axis=-1)
    onehot = (labels[:, :, None] == jnp.arange(num_classes)[None, None, :]).astype(jnp.float32)
    logit_err = (task_probs - onehot).astype(jnp.bfloat16)
    d_trunk = jnp.einsum("tbc,tdc->tbd", logit_err, task_heads, preferred_element_type=jnp.float32).astype(jnp.bfloat16)
    d_hidden = jnp.einsum("tbd,fd->tbf", d_trunk, w_two, preferred_element_type=jnp.float32)
    d_pre = (d_hidden * gelu_slope[None]).astype(jnp.bfloat16)
    part_b = jnp.einsum("cs,ucg->usg", low_rank, d_pre, preferred_element_type=jnp.float32)
    d_low = jnp.einsum("tbf,rf->tbr", d_pre, adapter_b, preferred_element_type=jnp.float32).astype(jnp.bfloat16)
    part_a = jnp.einsum("bd,tbr->tdr", tokens, d_low, preferred_element_type=jnp.float32)
    return part_a, part_b


def solution(mesh):
    num_dev = mesh.shape["data"]

    def device_step(tokens, labels, w_one, w_two, adapter_a, adapter_b, task_heads):
        batch_total = tokens.shape[0] * num_dev
        part_a, part_b = task_grads(tokens, labels, w_one, w_two, adapter_a, adapter_b, task_heads)
        shard_a = lax.psum_scatter(part_a, "data", scatter_dimension=1, tiled=True) / batch_total
        shard_b = lax.psum_scatter(part_b, "data", scatter_dimension=2, tiled=True) / batch_total
        gram_part = jnp.einsum("tdr,sdr->ts", shard_a, shard_a, precision=lax.Precision.HIGHEST) + jnp.einsum("usg,tsg->ut", shard_b, shard_b, precision=lax.Precision.HIGHEST)
        gram_mat = lax.psum(gram_part, "data")
        task_weights = weight_solver(gram_mat)
        comb_a = jnp.sum(task_weights[:, None, None] * shard_a, axis=0)
        comb_b = jnp.sum(task_weights[:, None, None] * shard_b, axis=0)
        return task_weights, comb_a, comb_b

    return jax.shard_map(device_step, mesh=mesh, in_specs=(P("data", None), P(None, "data"), P(), P(), P(), P(), P()), out_specs=(P(), P("data", None), P(None, "data")), check_vma=False)
```

profile of v0, /device:TPU:0, one launch (start us, length us, event | category | flops | bytes accessed | tf_op | source)
XLA Modules:
  0.0 397.3 jit_solution(8571244306520768661)
XLA Ops:
  7.2 1.4 convolution_convert_fusion.2
  8.7 7.0 %fusion.42 = f32[256,5120]{1,0:T(8,128)S(1)} fusion(bf16[256,1280]{1,0:T(8,128)(2,1)} %param.9, bf16[1280,5120]{1,0:T(8,128)(2,1)} %param.11), kind=kOutput, calls=%fused_computation.63 | convolution fusion | flops 3355443200 | bytes 19005440 | tf_op jit(solution)/shard_map/dot_general | solution.py:23
  15.7 5.1 %fusion.14 = (f32[256,5120]{1,0:T(8,128)}, f32[256,5120]{1,0:T(8,128)S(1)}) fusion(f32[256,5120]{1,0:T(8,128)S(1)} %fusion.42, bf16[256,8]{0,1:T(8,128)(2,1)S(1)} %convolution_convert_fusion.2, bf16[8,5120]{1,0:T(8,128)(2,1)S(1)} %copy-done.2), kind=kOutput, calls=%fused_computation.21 | convolution fusion | flops 43253760 | bytes 15814656 | tf_op jit(solution)/shard_map/dot_general | solution.py:23
  20.9 4.6 %fusion.20 = bf16[256,1280,1]{1,0,2:T(8,128)(2,1)S(1)} fusion(bf16[5120,1280]{1,0:T(8,128)(2,1)S(1)} %bitcast.52, f32[256,5120]{1,0:T(8,128)S(1)} %get-tuple-element.52, bf16[256,1280]{1,0:T(8,128)(2,1)S(1)} %copy-done.1), kind=kOutput, calls=%fused_computation.30 | convolution fusion | flops 3368222720 | bytes 19660800 | tf_op jit(solution)/shard_map/dot_general | solution.py:26
  25.8 17.2 %multiply_convert_fusion = bf16[3,256,5120]{2,1,0:T(8,128)(2,1)} fusion(bf16[5120,1280]{1,0:T(8,128)(2,1)} %param.12, f32[256,5120]{1,0:T(8,128)} %get-tuple-element.51, bf16[3,1280,13]{1,2,0:T(8,128)(2,1)S(1)} %copy-done, f32[3,256,13]{1,2,0:T(8,128)S(1)} %convolution_bitcast_fusion.2, s32[3,256]{1,0:T(4,128)S(1)} %copy-done.4, f32[3,256]{1,0:T(4,128)S(1)} %fusion.41), kind=kOutput, calls=%fused_computation.5 | convolution fusion | flops 10100796416 | bytes 26360320 | tf_op jit(solution)/shard_map/tbd,fd->tbf/dot_general | solution.py:32
  43.1 6.3 %convolution_bitcast_fusion.1 = f32[3,1280,8]{1,2,0:T(8,128)} fusion(bf16[3,256,5120]{2,1,0:T(8,128)(2,1)} %multiply_convert_fusion, bf16[256,1280]{1,0:T(8,128)(2,1)S(1)} %copy-done.1, bf16[8,5120]{1,0:T(8,128)(2,1)S(1)} %copy-done.2), kind=kOutput, calls=%fused_computation.31 | convolution fusion | flops 78649344 | bytes 8724480 | tf_op jit(solution)/shard_map/bd,tbr->tdr/dot_general | solution.py:36
  49.6 4.4 %convolution_bitcast_fusion = f32[3,8,5120]{2,1,0:T(8,128)S(1)} fusion(bf16[3,256,5120]{2,1,0:T(8,128)(2,1)} %multiply_convert_fusion, bf16[256,8]{0,1:T(8,128)(2,1)S(1)} %convolution_convert_fusion.2), kind=kOutput, calls=%fused_computation.11 | convolution fusion | flops 62914560 | bytes 8359936 | tf_op jit(solution)/shard_map/cs,ucg->usg/dot_general | solution.py:34
  54.0 6.5 %copy.20 = f32[3,8,5120]{1,0,2:T(4,128)} copy(f32[3,8,5120]{2,1,0:T(8,128)S(1)} %convolution_bitcast_fusion) | data formatting | bytes 983040
  60.5 10.9 %reshape.21 = f32[5120,24]{1,0:T(8,128)} reshape(f32[5120,3,8]{2,1,0:T(4,128)} %bitcast.49) | data formatting | bytes 983040
  71.4 108.3 %all-reduce.3.cloned.1.call-done = f32[3,1280,8]{1,2,0:T(8,128)} async-done(((f32[3,1280,8]{1,2,0:T(8,128)}), f32[3,1280,8]{1,2,0:T(8,128)}) %all-reduce.3.cloned.1.call-update) | async-done | bytes 122896
  179.8 0.8 dynamic-slice_multiply_fusion
  180.6 139.7 %reduce-scatter.5.cloned.1.call-done = f32[160,24]{1,0:T(8,128)} async-done(((f32[5120,24]{1,0:T(8,128)}), f32[160,24]{1,0:T(8,128)}) %reduce-scatter.5.cloned.1.call-update) | async-done | bytes 15376
  320.2 1.1 reshape.22
  321.9 36.9 %psum.7 = f32[3,3]{1,0:T(4,128)S(1)} all-reduce(f32[3,3]{1,0:T(4,128)S(1)} %fusion.23), channel_id=1, replica_groups=mesh['data'=32] {'data'}, use_global_device_ids=true, to_apply=%region_4.0 | all-reduce | flops 9 | bytes 72 | tf_op jit(solution)/shard_map/psum | solution.py:49
  360.0 28.4 %while.11 = (s32[]{:T(128)}, f32[3]{0:T(128)S(1)}, f32[3,3]{1,0:T(4,128)S(1)}, f32[]{:T(128)}, s32[]{:T(128)}, /*index=5*/s32[]{:T(128)}) while((s32[]{:T(128)}, f32[3]{0:T(128)S(1)}, f32[3,3]{1,0:T(4,128)S(1)}, f32[]{:T(128)}, s32[]{:T(128)}, /*index=5*/s32[]{:T(128)}) %tuple.30), condition=%wide.region_9.10_spmd.clone, body=%wide.region_6.9_spmd.clone.sunk | while | flops 38 | bytes 236 | solution.py:17
  360.2 0.6 fusion.58
  360.8 0.6 broadcast_divide_fusion.2
  361.6 0.6 fusion.58
  362.2 0.6 broadcast_divide_fusion.2
  363.0 0.6 fusion.58
  363.6 0.6 broadcast_divide_fusion.2
  365.0 0.6 broadcast_divide_fusion.2
  365.8 0.6 fusion.58
  366.4 0.6 broadcast_divide_fusion.2
  367.3 0.6 fusion.58
  367.9 0.6 broadcast_divide_fusion.2
  369.3 0.6 broadcast_divide_fusion.2
  370.1 0.6 fusion.58
  370.7 0.6 broadcast_divide_fusion.2
  371.5 0.6 fusion.58
  372.1 0.6 broadcast_divide_fusion.2
  373.5 0.6 broadcast_divide_fusion.2
  374.3 0.6 fusion.58
  375.0 0.6 broadcast_divide_fusion.2
  375.8 0.6 fusion.58
  376.4 0.6 broadcast_divide_fusion.2
  377.2 0.6 fusion.58
  377.8 0.6 broadcast_divide_fusion.2
  378.6 0.6 fusion.58
  379.2 0.6 broadcast_divide_fusion.2
  380.6 0.6 broadcast_divide_fusion.2
  382.1 0.6 broadcast_divide_fusion.2
  383.5 0.6 broadcast_divide_fusion.2
  384.9 0.6 broadcast_divide_fusion.2
  386.3 0.6 broadcast_divide_fusion.2
  387.7 0.6 broadcast_divide_fusion.2
  388.4 0.7 multiply_reduce_fusion.1
  389.1 1.4 multiply_reduce_fusion.2
  (81 shorter events, 10.0 us)
Async XLA Ops:
  7.2 18.3 %copy-start = (bf16[3,1280,13]{1,2,0:T(8,128)(2,1)S(1)}, bf16[3,1280,13]{1,2,0:T(8,128)(2,1)}, u32[]{:S(2)}) copy-start(bf16[3,1280,13]{1,2,0:T(8,128)(2,1)} %param.15) | copy-start | bytes 299524
  7.2 172.6 %all-reduce.3.cloned.1.call-start = ((), (), s32[]{:S(2)}) async-start(), calls=%async_computation.2 | async-start | bytes 245760
  8.6 7.1 %copy-start.2 = (bf16[8,5120]{1,0:T(8,128)(2,1)S(1)}, bf16[8,5120]{1,0:T(8,128)(2,1)}, u32[]{:S(2)}) copy-start(bf16[8,5120]{1,0:T(8,128)(2,1)} %param.14) | copy-start | bytes 245764
  8.6 12.2 %slice-start = ((s8[13107200]{0:T(1024)(128)(4,1)}), s8[4194304]{0:T(1024)(128)(4,1)S(1)}, s32[]{:S(2)}) async-start(s8[13107200]{0:T(1024)(128)(4,1)} %bitcast.51), calls=%async_computation.3 | async-start | bytes 8388608
  8.6 12.2 %slice-start.1 = ((s8[13107200]{0:T(1024)(128)(4,1)}), s8[4194304]{0:T(1024)(128)(4,1)S(1)}, s32[]{:S(2)}) async-start(s8[13107200]{0:T(1024)(128)(4,1)} %bitcast.51), calls=%async_computation.4 | async-start | bytes 8388608
  15.7 5.2 %copy-start.1 = (bf16[256,1280]{1,0:T(8,128)(2,1)S(1)}, bf16[256,1280]{1,0:T(8,128)(2,1)}, u32[]{:S(2)}) copy-start(bf16[256,1280]{1,0:T(8,128)(2,1)} %param.9) | copy-start | bytes 1966084
  15.7 5.2 %slice-start.2 = ((s8[13107200]{0:T(1024)(128)(4,1)}), s8[4194304]{0:T(1024)(128)(4,1)S(1)}, s32[]{:S(2)}) async-start(s8[13107200]{0:T(1024)(128)(4,1)} %bitcast.51), calls=%async_computation.5 | async-start | bytes 8388608
  15.7 5.2 %slice-start.3 = ((s8[13107200]{0:T(1024)(128)(4,1)}), s8[524288]{0:T(1024)(128)(4,1)S(1)}, s32[]{:S(2)}) async-start(s8[13107200]{0:T(1024)(128)(4,1)} %bitcast.51), calls=%async_computation.6 | async-start | bytes 1048576
  20.9 5.0 %copy-start.4 = (s32[3,256]{1,0:T(4,128)S(1)}, s32[3,256]{1,0:T(4,128)}, u32[]{:S(2)}) copy-start(s32[3,256]{1,0:T(4,128)} %param.10) | copy-start | bytes 9220
  49.4 270.8 %reduce-scatter.5.cloned.1.call-start = ((), (), s32[]{:S(2)}) async-start(), calls=%async_computation.1 | async-start | bytes 2703360
  388.4 2.1 copy-start.3
Sparse Core Ops, SparseCore 0:
  49.5 130.1 all-reduce.2
  182.0 138.1 reduce-scatter.4
where the time goes:
time: 399 us; the launch traced here: 397 us
  waiting for transfers between devices  248 us (62%)
  matrix products  46.7 us (12%)
  blocking collectives  36.9 us (9%)
  other arithmetic  31.3 us (8%)
  local copies, waits for them, and re-layouts  18.7 us (5%)
  between operations  14.9 us (4%)
    unnamed x4, waiting for transfers between devices  248 us
    psum x1, blocking collectives, device_step(): gram_mat = lax.psum(gram_part, 'data')  36.9 us
    unnamed x22, local copies, waits for them, and re-layouts  18.7 us
    dot_general x1, matrix products, task_grads(): jnp.einsum('tbd,fd->tbf', d_trunk, w_two, preferred_element_type=jnp.floa...  17.2 us
    div x20, other arithmetic, eg_step(): return weights / jnp.sum(weights)  13 us
    reduce_sum x20, other arithmetic, eg_step(): return weights / jnp.sum(weights)  12.4 us
  transfers between devices with their start and end apart: 2, of which 2 were waited for; matrix products, arithmetic and copies ran while one was open for 6% of the time, Pallas kernels for 0%

commit v1 on v0

--- a/solution.py
+++ b/solution.py
@@ -1,20 +1,14 @@
+import functools
+
 import jax
 import jax.numpy as jnp
 from jax import lax
+from jax.experimental import pallas as pl
+from jax.experimental.pallas import tpu as pltpu
 from jax.sharding import PartitionSpec as P
 
 EG_STEPS = 20
-
-
-def weight_solver(gram_mat):
-    num_tasks = gram_mat.shape[0]
-    eg_scale = jnp.trace(gram_mat) / num_tasks
-
-    def eg_step(step_idx, weights):
-        weights = weights * jnp.exp(-jnp.sum(gram_mat * weights[None, :], axis=1) / eg_scale)
-        return weights / jnp.sum(weights)
-
-    return lax.fori_loop(0, EG_STEPS, eg_step, jnp.full((num_tasks,), 1.0 / num_tasks, jnp.float32))
+MESH = pl.DeviceIdType.MESH
 
 
 def task_grads(tokens, labels, w_one, w_two, adapter_a, adapter_b, task_heads):
@@ -37,19 +31,160 @@
     return part_a, part_b
 
 
+def pack_parts(part_a, part_b, num_dev):
+    main_b = part_b.reshape(3, 8, num_dev, 160)
+    rem_b = main_b[..., 128:].transpose(2, 1, 0, 3).reshape(num_dev, 1, 8, 96)
+    main_b = main_b[..., :128].transpose(2, 0, 1, 3)
+    rows_a = part_a.reshape(3, num_dev, 5, 8, 8).transpose(1, 3, 2, 0, 4).reshape(num_dev, 1, 8, 120)
+    rem_b = jnp.pad(rem_b, ((0, 0), (0, 0), (0, 0), (0, 32)))
+    rows_a = jnp.pad(rows_a, ((0, 0), (0, 0), (0, 0), (0, 8)))
+    return jnp.concatenate([main_b, rem_b, rows_a], axis=1)
+
+
+def full_sum(tile):
+    return jnp.sum(jnp.sum(tile, axis=0, keepdims=True), axis=1, keepdims=True)
+
+
+def local_gram(main, rem, rows):
+    lane = lax.broadcasted_iota(jnp.int32, (8, 128), 1)
+    rem_task = lane // 32
+    row_task = (lane % 24) // 8
+    rem_1, rem_2 = pltpu.roll(rem, 96, 1), pltpu.roll(rem, 64, 1)
+    row_1, row_2 = pltpu.roll(rows, 120, 1), pltpu.roll(rows, 112, 1)
+
+    def entry(t, s, rem_other, row_other):
+        tile = main[t] * main[s]
+        tile = tile + jnp.where(rem_task == t, rem * rem_other, 0.0)
+        return full_sum(tile + jnp.where(row_task == t, rows * row_other, 0.0))
+
+    entries = [entry(0, 0, rem, rows), entry(1, 1, rem, rows), entry(2, 2, rem, rows)]
+    entries += [entry(0, 1, rem_1, row_1), entry(1, 2, rem_1, row_1), entry(0, 2, rem_2, row_2)]
+    lane_row = lax.broadcasted_iota(jnp.int32, (1, 128), 1)
+    gram_row = jnp.zeros((1, 128), jnp.float32)
+    for k, value in enumerate(entries):
+        gram_row = jnp.where(lane_row == k, value, gram_row)
+    return gram_row
+
+
+def solve_weights(gram_row):
+    lane_row = lax.broadcasted_iota(jnp.int32, (1, 128), 1)
+    m00, m11, m22, m01, m12, m02 = [jnp.sum(jnp.where(lane_row == k, gram_row, 0.0), axis=1, keepdims=True) for k in range(6)]
+    scale = (m00 + m11 + m22) / 3.0
+
+    def eg_step(_, w):
+        w0, w1, w2 = w
+        w0, w1, w2 = (
+            w0 * jnp.exp(-(m00 * w0 + m01 * w1 + m02 * w2) / scale),
+            w1 * jnp.exp(-(m01 * w0 + m11 * w1 + m12 * w2) / scale),
+            w2 * jnp.exp(-(m02 * w0 + m12 * w1 + m22 * w2) / scale),
+        )
+        total = w0 + w1 + w2
+        return w0 / total, w1 / total, w2 / total
+
+    third = jnp.full((1, 1), 1.0 / 3.0, jnp.float32)
+    return lax.fori_loop(0, EG_STEPS, eg_step, (third, third, third))
+
+
+def write_shares(weights, main, rem, rows, alpha_ref, ga_ref, gb_ref):
+    w0, w1, w2 = weights
+    lane_row = lax.broadcasted_iota(jnp.int32, (1, 128), 1)
+    alpha_ref[...] = jnp.where(lane_row == 0, w0, jnp.where(lane_row == 1, w1, w2))
+    lane = lax.broadcasted_iota(jnp.int32, (8, 128), 1)
+    rem_task, row_task = lane // 32, (lane % 24) // 8
+    gb_ref[:, 0:128] = w0 * main[0] + w1 * main[1] + w2 * main[2]
+    rem = rem * jnp.where(rem_task == 0, w0, jnp.where(rem_task == 1, w1, w2))
+    rem = rem + pltpu.roll(rem, 96, 1) + pltpu.roll(rem, 64, 1)
+    gb_ref[:, 128:160] = rem[:, 0:32]
+    rows = rows * jnp.where(row_task == 0, w0, jnp.where(row_task == 1, w1, w2))
+    rows = rows + pltpu.roll(rows, 120, 1) + pltpu.roll(rows, 112, 1)
+    for k in range(5):
+        piece = rows if k == 0 else pltpu.roll(rows, 128 - 24 * k, 1)
+        ga_ref[8 * k : 8 * k + 8, :] = piece[:, 0:8]
+
+
+def exchange_kernel(n, tok_total, parts_ref, alpha_ref, ga_ref, gb_ref, recv, gram_send, gram_recv, send_sem, recv_sem, gsend_sem, grecv_sem):
+    me = lax.axis_index("data")
+    barrier = pltpu.get_barrier_semaphore()
+
+    def greet(k, carry):
+        pl.semaphore_signal(barrier, inc=1, device_id=(lax.rem(me + k, n),), device_id_type=MESH)
+        return carry
+
+    lax.fori_loop(1, n, greet, 0)
+    pl.semaphore_wait(barrier, n - 1)
+
+    def send(k, carry):
+        dest = lax.rem(me + k, n)
+        pltpu.make_async_remote_copy(
+            src_ref=parts_ref.at[dest], dst_ref=recv.at[me], send_sem=send_sem, recv_sem=recv_sem,
+            device_id=(dest,), device_id_type=MESH,
+        ).start()
+        return carry
+
+    lax.fori_loop(1, n, send, 0)
+    recv[me] = parts_ref[me]
+    everyone = pltpu.make_async_remote_copy(
+        src_ref=parts_ref.at[pl.ds(0, n - 1)], dst_ref=recv.at[pl.ds(0, n - 1)], send_sem=send_sem, recv_sem=recv_sem,
+        device_id=(lax.rem(me + 1, n),), device_id_type=MESH,
+    )
+    everyone.wait_recv()
+    share = jnp.sum(recv[...], axis=0) / tok_total
+    main, rem, rows = (share[0], share[1], share[2]), share[3], share[4]
+    gram_row = local_gram(main, rem, rows)
+    gram_send[...] = gram_row
+    gram_recv[me] = gram_row
+
+    def send_gram(k, carry):
+        dest = lax.rem(me + k, n)
+        pltpu.make_async_remote_copy(
+            src_ref=gram_send, dst_ref=gram_recv.at[me], send_sem=gsend_sem, recv_sem=grecv_sem,
+            device_id=(dest,), device_id_type=MESH,
+        ).start()
+        return carry
+
+    lax.fori_loop(1, n, send_gram, 0)
+    every_gram = pltpu.make_async_remote_copy(
+        src_ref=gram_recv.at[pl.ds(0, n - 1)], dst_ref=gram_recv.at[pl.ds(0, n - 1)], send_sem=gsend_sem, recv_sem=grecv_sem,
+        device_id=(lax.rem(me + 1, n),), device_id_type=MESH,
+    )
+    every_gram.wait_recv()
+    weights = solve_weights(jnp.sum(gram_recv[...], axis=0))
+    write_shares(weights, main, rem, rows, alpha_ref, ga_ref, gb_ref)
+    everyone.wait_send()
+    every_gram.wait_send()
+
+
+def exchange(parts, num_dev, tok_total):
+    vmem = pl.BlockSpec(memory_space=pltpu.VMEM)
+    return pl.pallas_call(
+        functools.partial(exchange_kernel, num_dev, tok_total),
+        out_shape=(
+            jax.ShapeDtypeStruct((1, 128), jnp.float32),
+            jax.ShapeDtypeStruct((40, 8), jnp.float32),
+            jax.ShapeDtypeStruct((8, 160), jnp.float32),
+        ),
+        in_specs=[vmem],
+        out_specs=(vmem, vmem, vmem),
+        scratch_shapes=[
+            pltpu.VMEM((num_dev, 5, 8, 128), jnp.float32),
+            pltpu.VMEM((1, 128), jnp.float32),
+            pltpu.VMEM((num_dev, 1, 128), jnp.float32),
+            pltpu.SemaphoreType.DMA,
+            pltpu.SemaphoreType.DMA,
+            pltpu.SemaphoreType.DMA,
+            pltpu.SemaphoreType.DMA,
+        ],
+        compiler_params=pltpu.CompilerParams(collective_id=0, has_side_effects=True),
+        name="grad_exchange",
+    )(parts)
+
+
 def solution(mesh):
     num_dev = mesh.shape["data"]
 
     def device_step(tokens, labels, w_one, w_two, adapter_a, adapter_b, task_heads):
-        batch_total = tokens.shape[0] * num_dev
         part_a, part_b = task_grads(tokens, labels, w_one, w_two, adapter_a, adapter_b, task_heads)
-        shard_a = lax.psum_scatter(part_a, "data", scatter_dimension=1, tiled=True) / batch_total
-        shard_b = lax.psum_scatter(part_b, "data", scatter_dimension=2, tiled=True) / batch_total
-        gram_part = jnp.einsum("tdr,sdr->ts", shard_a, shard_a, precision=lax.Precision.HIGHEST) + jnp.einsum("usg,tsg->ut", shard_b, shard_b, precision=lax.Precision.HIGHEST)
-        gram_mat = lax.psum(gram_part, "data")
-        task_weights = weight_solver(gram_mat)
-        comb_a = jnp.sum(task_weights[:, None, None] * shard_a, axis=0)
-        comb_b = jnp.sum(task_weights[:, None, None] * shard_b, axis=0)
-        return task_weights, comb_a, comb_b
+        alpha, comb_a, comb_b = exchange(pack_parts(part_a, part_b, num_dev), num_dev, float(tokens.shape[0] * num_dev))
+        return alpha[0, :3], comb_a, comb_b
 
     return jax.shard_map(device_step, mesh=mesh, in_specs=(P("data", None), P(None, "data"), P(), P(), P(), P(), P()), out_specs=(P(), P("data", None), P(None, "data")), check_vma=False)

time: 399 us -> 90.2 us (0.23)
  waiting for transfers between devices: 248 us -> 0 us
  blocking collectives: 36.9 us -> 0 us
  Pallas kernels: 0 us -> 31.6 us
  other arithmetic: 31.3 us -> 1.97 us
  between operations: 14.9 us -> 0.81 us
  local copies, waits for them, and re-layouts: 18.7 us -> 9.73 us
    unnamed x4 -> x0, waiting for transfers between devices: 248 us -> none
    psum x1 -> x0, blocking collectives: 36.9 us -> none  [device_step(): gram_mat = lax.psum(gram_part, 'data')]
    pallas_call x0 -> x1, Pallas kernels: none -> 31.6 us  [exchange(): pl.pallas_call(functools.partial(exchange_kernel, num_dev, tok_total), ou...]
    reduce_sum x43 -> x0, other arithmetic: 17.4 us -> none  [the longest x20 12.4 us: eg_step(): return weights / jnp.sum(weights)]
    unnamed x22 -> x19, local copies, waits for them, and re-layouts: 18.7 us -> 3.77 us
    div x22 -> x0, other arithmetic: 13.8 us -> none  [the longest x20 13 us: eg_step(): return weights / jnp.sum(weights)]
  transfers between devices with their start and end apart: 2 -> 0, of which waited for: 2 -> 0; matrix products, arithmetic and copies ran while one was open for 6% -> 0% of each run, Pallas kernels for 0% -> 0%
where the time goes in v1:
time: 90.2 us; the launch traced here: 89.7 us
  matrix products  45.6 us (51%)
  Pallas kernels  31.6 us (35%)
  local copies, waits for them, and re-layouts  9.73 us (11%)
  other arithmetic  1.97 us (2%)
    pallas_call x1, Pallas kernels, exchange(): pl.pallas_call(functools.partial(exchange_kernel, num_dev, tok_total), ou...  31.6 us
    dot_general x1, matrix products, task_grads(): jnp.einsum('tbd,fd->tbf', d_trunk, w_two, preferred_element_type=jnp.floa...  17.3 us
    dot_general x1, matrix products, task_grads(): jnp.dot(tokens, w_one, preferred_element_type=jnp.float32)  6.96 us
    dot_general x1, matrix products, task_grads(): jnp.einsum('bd,tbr->tdr', tokens, d_low, preferred_element_type=jnp.float32)  5.64 us
    dot_general x1, matrix products, task_grads(): jnp.dot(low_rank, adapter_b, preferred_element_type=jnp.float32)  5.11 us
    dot_general x1, matrix products, task_grads(): jnp.dot(hidden, w_two, preferred_element_type=jnp.float32)  4.57 us
    dot_general x1, matrix products, task_grads(): jnp.einsum('cs,ucg->usg', low_rank, d_pre, preferred_element_type=jnp.flo...  4.39 us
    unnamed x19, local copies, waits for them, and re-layouts  3.77 us

profile of v1, /device:TPU:0, one launch (start us, length us, event | category | flops | bytes accessed | tf_op | source)
XLA Modules:
  0.0 89.7 jit_solution(11987543338539418961)
XLA Ops:
  0.6 0.0 copy-start
  0.6 1.4 %convolution_convert_fusion.2 = bf16[256,8]{0,1:T(8,128)(2,1)S(1)} fusion(bf16[256,1280]{1,0:T(8,128)(2,1)} %param.7, bf16[1280,8]{0,1:T(8,128)(2,1)} %param.11), kind=kOutput, calls=%fused_computation.32 | convolution fusion | flops 5244928 | bytes 679936 | tf_op jit(solution)/shard_map/dot_general | solution.py:16
  2.0 0.0 copy-start.2
  2.0 0.0 slice-start
  2.0 0.1 slice-start.1
  2.1 7.0 %fusion.39 = f32[256,5120]{1,0:T(8,128)S(1)} fusion(bf16[256,1280]{1,0:T(8,128)(2,1)} %param.7, bf16[1280,5120]{1,0:T(8,128)(2,1)} %param.9), kind=kOutput, calls=%fused_computation.55 | convolution fusion | flops 3355443200 | bytes 19005440 | tf_op jit(solution)/shard_map/dot_general | solution.py:17
  9.1 0.0 copy-done.2
  9.1 0.0 copy-start.1
  9.1 0.0 slice-start.2
  9.1 0.0 slice-start.3
  9.1 5.1 %fusion.14 = (f32[256,5120]{1,0:T(8,128)}, f32[256,5120]{1,0:T(8,128)S(1)}) fusion(f32[256,5120]{1,0:T(8,128)S(1)} %fusion.39, bf16[256,8]{0,1:T(8,128)(2,1)S(1)} %convolution_convert_fusion.2, bf16[8,5120]{1,0:T(8,128)(2,1)S(1)} %copy-done.2), kind=kOutput, calls=%fused_computation.17 | convolution fusion | flops 43253760 | bytes 15814656 | tf_op jit(solution)/shard_map/dot_general | solution.py:17
  14.2 0.0 slice-done
  14.2 0.0 slice-done.1
  14.2 0.0 copy-done.1
  14.2 0.0 slice-done.2
  14.2 0.0 slice-done.3
  14.3 0.0 copy-start.3
  14.3 4.6 %fusion.20 = bf16[256,1280,1]{1,0,2:T(8,128)(2,1)S(1)} fusion(bf16[5120,1280]{1,0:T(8,128)(2,1)S(1)} %bitcast.54, f32[256,5120]{1,0:T(8,128)S(1)} %get-tuple-element.16, bf16[256,1280]{1,0:T(8,128)(2,1)S(1)} %copy-done.1), kind=kOutput, calls=%fused_computation.26 | convolution fusion | flops 3368222720 | bytes 19660800 | tf_op jit(solution)/shard_map/dot_general | solution.py:20
  18.8 0.0 copy-done
  18.9 0.3 convolution_bitcast_fusion.2
  19.1 0.1 fusion.38
  19.2 0.0 copy-done.3
  19.2 17.3 %multiply_convert_fusion = bf16[3,256,5120]{2,1,0:T(8,128)(2,1)} fusion(bf16[5120,1280]{1,0:T(8,128)(2,1)} %param.10, f32[256,5120]{1,0:T(8,128)} %get-tuple-element.15, bf16[3,1280,13]{1,2,0:T(8,128)(2,1)S(1)} %copy-done, f32[3,256,13]{1,2,0:T(8,128)S(1)} %convolution_bitcast_fusion.2, s32[3,256]{1,0:T(4,128)S(1)} %copy-done.3, f32[3,256]{1,0:T(4,128)S(1)} %fusion.38), kind=kOutput, calls=%fused_computation.1 | convolution fusion | flops 10100796416 | bytes 26360320 | tf_op jit(solution)/shard_map/tbd,fd->tbf/dot_general | solution.py:26
  36.5 5.6 %convolution_bitcast_fusion.1 = f32[3,1280,8]{1,2,0:T(8,128)S(1)} fusion(bf16[3,256,5120]{2,1,0:T(8,128)(2,1)} %multiply_convert_fusion, bf16[256,1280]{1,0:T(8,128)(2,1)S(1)} %copy-done.1, bf16[8,5120]{1,0:T(8,128)(2,1)S(1)} %copy-done.2), kind=kOutput, calls=%fused_computation.27 | convolution fusion | flops 78649344 | bytes 8724480 | tf_op jit(solution)/shard_map/bd,tbr->tdr/dot_general | solution.py:30
  42.2 4.4 %convolution_bitcast_fusion = f32[3,8,5120]{2,1,0:T(8,128)S(1)} fusion(bf16[3,256,5120]{2,1,0:T(8,128)(2,1)} %multiply_convert_fusion, bf16[256,8]{0,1:T(8,128)(2,1)S(1)} %convolution_convert_fusion.2), kind=kOutput, calls=%fused_computation.7 | convolution fusion | flops 62914560 | bytes 8359936 | tf_op jit(solution)/shard_map/cs,ucg->usg/dot_general | solution.py:28
  46.6 0.4 reshape.22
  47.1 1.0 %copy.21 = f32[3,8,32,128]{3,1,0,2:T(8,128)} copy(f32[3,8,32,128]{3,2,1,0:T(8,128)S(1)} %slice.12) | data formatting | bytes 786432
  48.0 0.3 copy.14
  48.3 0.2 reshape.23
  48.5 0.9 %reshape.24 = f32[3,32,5,8,8]{3,2,1,4,0:T(8,128)S(1)} reshape(f32[3,1280,8]{1,2,0:T(8,128)S(1)} %convolution_bitcast_fusion.1) | data formatting | bytes 245760 | tf_op jit(solution)/shard_map/reshape | solution.py:38
  49.5 1.8 %copy.16 = f32[32,8,5,3,8]{0,4,3,2,1:T(8,128)} copy(f32[32,8,5,3,8]{1,2,0,4,3:T(8,128)S(1)} %bitcast.49) | data formatting | bytes 245760 | tf_op jit(solution)/shard_map/transpose | solution.py:38
  51.2 1.2 %copy.17 = f32[32,1,8,120]{3,2,1,0:T(8,128)S(1)} copy(f32[32,1,8,120]{0,3,2,1:T(8,128)} %bitcast.50) | data formatting | bytes 245760 | tf_op jit(solution)/shard_map/reshape | solution.py:38
  52.4 1.9 %select_maximum_fusion.parts_ref = f32[32,5,8,128]{3,2,1,0:T(8,128)} fusion(f32[32,1,8,120]{3,2,1,0:T(8,128)S(1)} %copy.17, f32[32,1,8,96]{3,2,1,0:T(8,128)S(1)} %bitcast.52, f32[32,3,8,128]{3,2,1,0:T(8,128)} %bitcast.51), kind=kLoop, calls=%fused_computation.35 | loop fusion | flops 1310720 | bytes 1269760 | tf_op jit(solution)/shard_map/concatenate | solution.py:41
  54.3 31.6 %grad_exchange.1 = (f32[1,128]{1,0:T(1,128)}, f32[40,8]{1,0:T(8,128)}, f32[8,160]{1,0:T(8,128)}) custom-call(f32[32,5,8,128]{3,2,1,0:T(8,128)} %select_maximum_fusion.parts_ref), custom_call_target="tpu_custom_call" | custom-call | tf_op jit(solution)/shard_map/grad_exchange/pallas_call | solution.py:159
  85.9 1.1 %slice_bitcast_fusion.1 = f32[3]{0:T(128)} fusion(f32[1,128]{1,0:T(1,128)} %get-tuple-element.6), kind=kLoop, calls=%fused_computation.48 | loop fusion | bytes 24 | tf_op jit(solution)/shard_map/squeeze | solution.py:188
  87.0 1.4 %copy.18 = f32[40,8]{0,1:T(8,128)} copy(f32[40,8]{1,0:T(8,128)} %get-tuple-element.13) | data formatting | bytes 2560
  88.4 1.3 %copy.23 = f32[8,160]{1,0:T(8,128)} copy(f32[8,160]{1,0:T(8,128)} %get-tuple-element.22) | data formatting | bytes 10240
  (3 shorter events, 0.1 us)
Async XLA Ops:
  0.6 18.2 %copy-start = (bf16[3,1280,13]{1,2,0:T(8,128)(2,1)S(1)}, bf16[3,1280,13]{1,2,0:T(8,128)(2,1)}, u32[]{:S(2)}) copy-start(bf16[3,1280,13]{1,2,0:T(8,128)(2,1)} %param.13) | copy-start | bytes 299524
  2.0 7.1 %copy-start.2 = (bf16[8,5120]{1,0:T(8,128)(2,1)S(1)}, bf16[8,5120]{1,0:T(8,128)(2,1)}, u32[]{:S(2)}) copy-start(bf16[8,5120]{1,0:T(8,128)(2,1)} %param.12) | copy-start | bytes 245764
  2.0 12.2 %slice-start = ((s8[13107200]{0:T(1024)(128)(4,1)}), s8[4194304]{0:T(1024)(128)(4,1)S(1)}, s32[]{:S(2)}) async-start(s8[13107200]{0:T(1024)(128)(4,1)} %bitcast.53), calls=%async_computation | async-start | bytes 8388608
  2.0 12.2 %slice-start.1 = ((s8[13107200]{0:T(1024)(128)(4,1)}), s8[4194304]{0:T(1024)(128)(4,1)S(1)}, s32[]{:S(2)}) async-start(s8[13107200]{0:T(1024)(128)(4,1)} %bitcast.53), calls=%async_computation.1 | async-start | bytes 8388608
  9.1 5.1 %copy-start.1 = (bf16[256,1280]{1,0:T(8,128)(2,1)S(1)}, bf16[256,1280]{1,0:T(8,128)(2,1)}, u32[]{:S(2)}) copy-start(bf16[256,1280]{1,0:T(8,128)(2,1)} %param.7) | copy-start | bytes 1966084
  9.1 5.1 %slice-start.2 = ((s8[13107200]{0:T(1024)(128)(4,1)}), s8[4194304]{0:T(1024)(128)(4,1)S(1)}, s32[]{:S(2)}) async-start(s8[13107200]{0:T(1024)(128)(4,1)} %bitcast.53), calls=%async_computation.2 | async-start | bytes 8388608
  9.1 5.1 %slice-start.3 = ((s8[13107200]{0:T(1024)(128)(4,1)}), s8[524288]{0:T(1024)(128)(4,1)S(1)}, s32[]{:S(2)}) async-start(s8[13107200]{0:T(1024)(128)(4,1)} %bitcast.53), calls=%async_computation.3 | async-start | bytes 1048576
  14.3 5.0 %copy-start.3 = (s32[3,256]{1,0:T(4,128)S(1)}, s32[3,256]{1,0:T(4,128)}, u32[]{:S(2)}) copy-start(s32[3,256]{1,0:T(4,128)} %param.8) | copy-start | bytes 9220

commit v2 on v1

v2 whole, which is shorter than its diff:
```python
import functools

import jax
import jax.numpy as jnp
from jax import lax
from jax.experimental import pallas as pl
from jax.experimental.pallas import tpu as pltpu
from jax.sharding import PartitionSpec as P

EG_STEPS = 20
FWD_COLS = 512
BWD_COLS = 1280
NUM_TASKS = 3
PLANE = 8
GELU_SCALE = 0.7978845608028654
GELU_CUBE = 0.044715
MESH = pl.DeviceIdType.MESH


def full_sum(tile):
    return jnp.sum(jnp.sum(tile, axis=0, keepdims=True), axis=1, keepdims=True)


def local_gram(main, rem, rows):
    lane = lax.broadcasted_iota(jnp.int32, (8, 128), 1)
    rem_task = lane // 32
    row_task = (lane % 24) // 8
    rem_1, rem_2 = pltpu.roll(rem, 96, 1), pltpu.roll(rem, 64, 1)
    row_1, row_2 = pltpu.roll(rows, 120, 1), pltpu.roll(rows, 112, 1)

    def entry(t, s, rem_other, row_other):
        tile = main[t] * main[s]
        tile = tile + jnp.where(rem_task == t, rem * rem_other, 0.0)
        return full_sum(tile + jnp.where(row_task == t, rows * row_other, 0.0))

    entries = [entry(0, 0, rem, rows), entry(1, 1, rem, rows), entry(2, 2, rem, rows)]
    entries += [entry(0, 1, rem_1, row_1), entry(1, 2, rem_1, row_1), entry(0, 2, rem_2, row_2)]
    lane_row = lax.broadcasted_iota(jnp.int32, (1, 128), 1)
    gram_row = jnp.zeros((1, 128), jnp.float32)
    for k, value in enumerate(entries):
        gram_row = jnp.where(lane_row == k, value, gram_row)
    return gram_row


def solve_weights(gram_row):
    lane_row = lax.broadcasted_iota(jnp.int32, (1, 128), 1)
    m00, m11, m22, m01, m12, m02 = [jnp.sum(jnp.where(lane_row == k, gram_row, 0.0), axis=1, keepdims=True) for k in range(6)]
    scale = (m00 + m11 + m22) / 3.0

    def eg_step(_, w):
        w0, w1, w2 = w
        w0, w1, w2 = (
            w0 * jnp.exp(-(m00 * w0 + m01 * w1 + m02 * w2) / scale),
            w1 * jnp.exp(-(m01 * w0 + m11 * w1 + m12 * w2) / scale),
            w2 * jnp.exp(-(m02 * w0 + m12 * w1 + m22 * w2) / scale),
        )
        total = w0 + w1 + w2
        return w0 / total, w1 / total, w2 / total

    third = jnp.full((1, 1), 1.0 / 3.0, jnp.float32)
    return lax.fori_loop(0, EG_STEPS, eg_step, (third, third, third))


def write_shares(weights, main, rem, rows, alpha_ref, ga_ref, gb_ref):
    w0, w1, w2 = weights
    lane_row = lax.broadcasted_iota(jnp.int32, (1, 128), 1)
    alpha_ref[...] = jnp.where(lane_row == 0, w0, jnp.where(lane_row == 1, w1, w2))
    lane = lax.broadcasted_iota(jnp.int32, (8, 128), 1)
    rem_task, row_task = lane // 32, (lane % 24) // 8
    gb_ref[:, 0:128] = w0 * main[0] + w1 * main[1] + w2 * main[2]
    rem = rem * jnp.where(rem_task == 0, w0, jnp.where(rem_task == 1, w1, w2))
    rem = rem + pltpu.roll(rem, 96, 1) + pltpu.roll(rem, 64, 1)
    gb_ref[:, 128:160] = rem[:, 0:32]
    rows = rows * jnp.where(row_task == 0, w0, jnp.where(row_task == 1, w1, w2))
    rows = rows + pltpu.roll(rows, 120, 1) + pltpu.roll(rows, 112, 1)
    for k in range(5):
        piece = rows if k == 0 else pltpu.roll(rows, 128 - 24 * k, 1)
        ga_ref[8 * k : 8 * k + 8, :] = piece[:, 0:8]


def dot_t(lhs, rhs):
    return lax.dot_general(lhs, rhs, (((1,), (1,)), ((), ())), preferred_element_type=jnp.float32)


def dot_n(lhs, rhs):
    return jnp.dot(lhs, rhs, preferred_element_type=jnp.float32)


def gelu_and_slope(pre_act):
    square = pre_act * pre_act
    tanh = jnp.tanh(GELU_SCALE * pre_act * (1.0 + GELU_CUBE * square))
    cdf = 0.5 + 0.5 * tanh
    bell = (0.5 * GELU_SCALE) * (1.0 - tanh * tanh) * (1.0 + (3.0 * GELU_CUBE) * square)
    return pre_act * cdf, cdf + pre_act * bell


def logit_errors(logits, labels, num_classes):
    by_class = logits.T
    errors = []
    for t in range(NUM_TASKS):
        rows = by_class[16 * t : 16 * t + 16, :]
        cls = lax.broadcasted_iota(jnp.int32, rows.shape, 0)
        rows = jnp.where(cls < num_classes, rows, -jnp.inf)
        expo = jnp.exp(rows - jnp.max(rows, axis=0, keepdims=True))
        probs = expo / jnp.sum(expo, axis=0, keepdims=True)
        errors.append(probs - jnp.where(cls == labels[t : t + 1, :], 1.0, 0.0))
    errors.append(jnp.zeros((128 - 16 * NUM_TASKS, logits.shape[0]), jnp.float32))
    return jnp.concatenate(errors, axis=0).T


def pack_share_columns(main_cols, dest):
    first = 160 * dest // 128
    shift = 160 * dest - 128 * first
    main, rem = [], []
    for cols in main_cols:
        left = cols[:, 128 * first : 128 * first + 128]
        right = cols[:, 128 * first + 128 : 128 * first + 256]
        lane = lax.broadcasted_iota(jnp.int32, left.shape, 1)
        if shift == 0:
            main.append(left)
            rem.append(right)
        else:
            left, right = pltpu.roll(left, 128 - shift, 1), pltpu.roll(right, 128 - shift, 1)
            main.append(jnp.where(lane < 128 - shift, left, right))
            rem.append(right)
    lane = lax.broadcasted_iota(jnp.int32, (8, 128), 1)
    tail = jnp.where(lane < 32, rem[0], 0.0)
    tail = jnp.where(lane // 32 == 1, pltpu.roll(rem[1], 32, 1), tail)
    tail = jnp.where(lane // 32 == 2, pltpu.roll(rem[2], 64, 1), tail)
    return main, tail


def step_kernel(
    n, tok_total, num_classes,
    x_hbm, y_hbm, w1_hbm, w2_hbm, a_hbm, bm_hbm, heads_hbm,
    alpha_ref, ga_ref, gb_ref,
    x, y, w1, w2, a, bm, heads, slope, z_acc, x_t, u_t, hcat, err, dz, dp, du_t,
    send_b, recv_b, sum_b, recv_z, send_a, recv_a, gram_send, gram_recv,
    in_sem, w1_sem, w2_sem, bsend_sem, brecv_sem, zsend_sem, zrecv_sem, asend_sem, arecv_sem, gsend_sem, grecv_sem,
):
    me = lax.axis_index("data")
    plane, spot = me // PLANE, me % PLANE
    planes = n // PLANE
    d_model, d_ff = w1_hbm.shape
    toks = x_hbm.shape[0]
    fwd_steps = d_ff // FWD_COLS

    small = [
        pltpu.make_async_copy(src, dst, in_sem.at[k])
        for k, (src, dst) in enumerate([(x_hbm, x), (a_hbm, a), (bm_hbm, bm), (heads_hbm, heads), (y_hbm, y)])
    ]

    def w1_copy(j):
        return pltpu.make_async_copy(w1_hbm.at[:, pl.ds(pl.multiple_of(j * FWD_COLS, FWD_COLS), FWD_COLS)], w1.at[j], w1_sem.at[j])

    def w2_copy(j):
        rows = pl.ds(pl.multiple_of(j * FWD_COLS, FWD_COLS), FWD_COLS)
        return pltpu.make_async_copy(w2_hbm.at[rows, :], w2.at[rows, :], w2_sem.at[j])

    for copy in small:
        copy.start()

    def fetch(j, carry):
        w1_copy(j).start()
        w2_copy(j).start()
        return carry

    lax.fori_loop(0, fwd_steps, fetch, 0)

    barrier = pltpu.get_barrier_semaphore()

    def greet(k, carry):
        pl.semaphore_signal(barrier, inc=1, device_id=(lax.rem(me + k, n),), device_id_type=MESH)
        return carry

    lax.fori_loop(1, n, greet, 0)

    for copy in small:
        copy.wait()
    low_rank = dot_n(x[...], a[...])
    u_t[...] = low_rank.T.astype(jnp.bfloat16)
    low_rank = low_rank.astype(jnp.bfloat16)
    x_t[...] = x[...].astype(jnp.float32).T.astype(jnp.bfloat16)
    placed = jnp.zeros((d_model, 128), jnp.float32)
    for t in range(NUM_TASKS):
        cls = lax.broadcasted_iota(jnp.int32, (num_classes, 128), 0)
        lane = lax.broadcasted_iota(jnp.int32, (num_classes, 128), 1)
        place = jnp.where(lane == cls + 16 * t, 1.0, 0.0).astype(jnp.bfloat16)
        placed = placed + dot_n(heads[t], place)
    hcat[...] = placed.astype(jnp.bfloat16)
    z_acc[...] = jnp.zeros_like(z_acc)

    def forward(j, carry):
        cols = pl.ds(pl.multiple_of(j * FWD_COLS, FWD_COLS), FWD_COLS)
        w1_copy(j).wait()
        w2_copy(j).wait()
        pre_act = dot_n(x[...], w1[j]) + dot_n(low_rank, bm[:, cols])
        act, slope_tile = gelu_and_slope(pre_act)
        slope[:, cols] = slope_tile
        z_acc[...] += dot_n(act.astype(jnp.bfloat16), w2[cols, :])
        return carry

    lax.fori_loop(0, fwd_steps, forward, 0)

    trunk = (x[...].astype(jnp.float32) + z_acc[...]).astype(jnp.bfloat16)
    errors = logit_errors(dot_n(trunk, hcat[...]), y[...], num_classes)
    lane = lax.broadcasted_iota(jnp.int32, (toks, 128), 1)
    for t in range(NUM_TASKS):
        err[pl.ds(t * toks, toks), :] = jnp.where(lane // 16 == t, errors, 0.0).astype(jnp.bfloat16)
    dz[...] = dot_t(err[...], hcat[...]).astype(jnp.bfloat16)
    du_t[...] = jnp.zeros_like(du_t)
    pl.semaphore_wait(barrier, n - 1)

    def plane_copy(i, to):
        return pltpu.make_async_remote_copy(
            src_ref=send_b.at[i, to], dst_ref=recv_b.at[i, spot], send_sem=bsend_sem, recv_sem=brecv_sem.at[i],
            device_id=(plane * PLANE + to,), device_id_type=MESH,
        )

    def plane_wait(i):
        pltpu.make_async_remote_copy(
            src_ref=send_b.at[i, pl.ds(0, PLANE - 1)], dst_ref=recv_b.at[i, pl.ds(0, PLANE - 1)], send_sem=bsend_sem, recv_sem=brecv_sem.at[i],
            device_id=(lax.rem(me + 1, n),), device_id_type=MESH,
        ).wait_recv()

    def backward(i, carry):
        chunk = lax.rem(plane + 1 + i, planes)
        cols = pl.ds(pl.multiple_of(chunk * BWD_COLS, BWD_COLS), BWD_COLS)
        d_hidden = dot_t(dz[...], w2[cols, :])
        slope_tile = slope[:, cols]
        for t in range(NUM_TASKS):
            dp[pl.ds(t * toks, toks), :] = (d_hidden[t * toks : (t + 1) * toks, :] * slope_tile).astype(jnp.bfloat16)
        du_t[...] += dot_t(bm[:, cols], dp[...])
        grads = [dot_n(u_t[...], dp[pl.ds(t * toks, toks), :]) for t in range(NUM_TASKS)]
        for to in range(PLANE):
            main, tail = pack_share_columns(grads, to)
            for t in range(NUM_TASKS):
                send_b[i, to, t] = main[t]
            send_b[i, to, NUM_TASKS] = tail

        def send(k, carry):
            plane_copy(i, lax.rem(spot + k, PLANE)).start()
            return carry

        lax.fori_loop(1, PLANE, send, 0)
        recv_b[i, spot] = send_b[i, spot]

        @pl.when(i >= 1)
        def _():
            before = i - 1
            plane_wait(before)
            sum_b[before] = jnp.sum(recv_b[before], axis=0)
            pltpu.make_async_remote_copy(
                src_ref=sum_b.at[before], dst_ref=recv_z.at[before], send_sem=zsend_sem, recv_sem=zrecv_sem,
                device_id=(lax.rem(plane + i, planes) * PLANE + spot,), device_id_type=MESH,
            ).start()

        return carry

    lax.fori_loop(0, planes, backward, 0)

    du = du_t[...]
    du_rep = jnp.concatenate([du[:, t * toks : (t + 1) * toks] for t in range(NUM_TASKS)] * 5 + [jnp.zeros((8, toks), jnp.float32)], axis=0)
    rows_a = dot_t(x_t[...], du_rep.astype(jnp.bfloat16)).reshape(n, 5, 8, 128)
    lane = lax.broadcasted_iota(jnp.int32, (n, 8, 128), 2)
    packed = jnp.zeros((n, 8, 128), jnp.float32)
    for k in range(5):
        packed = jnp.where(lane // 24 == k, rows_a[:, k], packed)
    send_a[...] = packed

    def a_copy(to):
        return pltpu.make_async_remote_copy(
            src_ref=send_a.at[to], dst_ref=recv_a.at[me], send_sem=asend_sem, recv_sem=arecv_sem,
            device_id=(to,), device_id_type=MESH,
        )

    def send_rows(k, carry):
        a_copy(lax.rem(me + k, n)).start()
        return carry

    lax.fori_loop(1, n, send_rows, 0)
    recv_a[me] = send_a[me]

    plane_wait(planes - 1)
    every_z = pltpu.make_async_remote_copy(
        src_ref=sum_b, dst_ref=recv_z, send_sem=zsend_sem, recv_sem=zrecv_sem, device_id=(lax.rem(me + 1, n),), device_id_type=MESH
    )
    every_z.wait_recv()
    share_b = (jnp.sum(recv_b[planes - 1], axis=0) + jnp.sum(recv_z[...], axis=0)) / tok_total
    main, rem = (share_b[0], share_b[1], share_b[2]), share_b[3]
    every_a = pltpu.make_async_remote_copy(
        src_ref=send_a.at[pl.ds(0, n - 1)], dst_ref=recv_a.at[pl.ds(0, n - 1)], send_sem=asend_sem, recv_sem=arecv_sem,
        device_id=(lax.rem(me + 1, n),), device_id_type=MESH,
    )
    every_a.wait_recv()
    rows = jnp.sum(recv_a[...], axis=0) / tok_total
    gram_row = local_gram(main, rem, rows)
    gram_send[...] = gram_row
    gram_recv[me] = gram_row

    def send_gram(k, carry):
        pltpu.make_async_remote_copy(
            src_ref=gram_send, dst_ref=gram_recv.at[me], send_sem=gsend_sem, recv_sem=grecv_sem,
            device_id=(lax.rem(me + k, n),), device_id_type=MESH,
        ).start()
        return carry

    lax.fori_loop(1, n, send_gram, 0)
    every_gram = pltpu.make_async_remote_copy(
        src_ref=gram_recv.at[pl.ds(0, n - 1)], dst_ref=gram_recv.at[pl.ds(0, n - 1)], send_sem=gsend_sem, recv_sem=grecv_sem,
        device_id=(lax.rem(me + 1, n),), device_id_type=MESH,
    )
    every_gram.wait_recv()
    weights = solve_weights(jnp.sum(gram_recv[...], axis=0))
    write_shares(weights, main, rem, rows, alpha_ref, ga_ref, gb_ref)
    pltpu.make_async_remote_copy(
        src_ref=send_b.at[:, pl.ds(0, PLANE - 1)], dst_ref=recv_b.at[:, pl.ds(0, PLANE - 1)], send_sem=bsend_sem, recv_sem=brecv_sem.at[0],
        device_id=(lax.rem(me + 1, n),), device_id_type=MESH,
    ).wait_send()
    every_z.wait_send()
    every_a.wait_send()
    every_gram.wait_send()


def solution(mesh):
    num_dev = mesh.shape["data"]

    def device_step(tokens, labels, w_one, w_two, adapter_a, adapter_b, task_heads):
        toks, d_model = tokens.shape
        d_ff = w_one.shape[1]
        fwd_steps = d_ff // FWD_COLS
        planes = num_dev // PLANE
        bf16, f32 = jnp.bfloat16, jnp.float32
        dma = pltpu.SemaphoreType.DMA
        vmem = pl.BlockSpec(memory_space=pltpu.VMEM)
        hbm = pl.BlockSpec(memory_space=pltpu.HBM)
        alpha, comb_a, comb_b = pl.pallas_call(
            functools.partial(step_kernel, num_dev, float(toks * num_dev), task_heads.shape[2]),
            out_shape=(
                jax.ShapeDtypeStruct((1, 128), f32),
                jax.ShapeDtypeStruct((d_model // num_dev, 8), f32),
                jax.ShapeDtypeStruct((8, d_ff // num_dev), f32),
            ),
            in_specs=[hbm] * 7,
            out_specs=(vmem, vmem, vmem),
            scratch_shapes=[
                pltpu.VMEM(tokens.shape, bf16),
                pltpu.VMEM(labels.shape, jnp.int32),
                pltpu.VMEM((fwd_steps, d_model, FWD_COLS), bf16),
                pltpu.VMEM(w_two.shape, bf16),
                pltpu.VMEM(adapter_a.shape, bf16),
                pltpu.VMEM(adapter_b.shape, bf16),
                pltpu.VMEM(task_heads.shape, bf16),
                pltpu.VMEM((toks, d_ff), f32),
                pltpu.VMEM((toks, d_model), f32),
                pltpu.VMEM((d_model, toks), bf16),
                pltpu.VMEM((8, toks), bf16),
                pltpu.VMEM((d_model, 128), bf16),
                pltpu.VMEM((NUM_TASKS * toks, 128), bf16),
                pltpu.VMEM((NUM_TASKS * toks, d_model), bf16),
                pltpu.VMEM((NUM_TASKS * toks, BWD_COLS), bf16),
                pltpu.VMEM((8, NUM_TASKS * toks), f32),
                pltpu.VMEM((planes, PLANE, 4, 8, 128), f32),
                pltpu.VMEM((planes, PLANE, 4, 8, 128), f32),
                pltpu.VMEM((planes - 1, 4, 8, 128), f32),
                pltpu.VMEM((planes - 1, 4, 8, 128), f32),
                pltpu.VMEM((num_dev, 8, 128), f32),
                pltpu.VMEM((num_dev, 8, 128), f32),
                pltpu.VMEM((1, 128), f32),
                pltpu.VMEM((num_dev, 1, 128), f32),
                dma((5,)),
                dma((fwd_steps,)),
                dma((fwd_steps,)),
                dma,
                dma((planes,)),
                dma,
                dma,
                dma,
                dma,
                dma,
                dma,
            ],
            compiler_params=pltpu.CompilerParams(collective_id=0, has_side_effects=True, vmem_limit_bytes=60 * 1024 * 1024),
            name="grad_step",
        )(tokens, labels, w_one, w_two, adapter_a, adapter_b, task_heads)
        return alpha[0, :3], comb_a, comb_b

    return jax.shard_map(device_step, mesh=mesh, in_specs=(P("data", None), P(None, "data"), P(), P(), P(), P(), P()), out_specs=(P(), P("data", None), P(None, "data")), check_vma=False)
```

time: 90.2 us -> 56.7 us (0.63)
  matrix products: 45.6 us -> 0 us
  Pallas kernels: 31.6 us -> 48.1 us
  local copies, waits for them, and re-layouts: 9.73 us -> 7.7 us
  other arithmetic: 1.97 us -> 0 us
    dot_general x8 -> x0, matrix products: 45.6 us -> none  [the longest x1 17.3 us: task_grads(): jnp.einsum('tbd,fd->tbf', d_trunk, w_two, preferred_element_type=jnp.floa...]
    pallas_call x1, Pallas kernels: 31.6 us -> 48.1 us  [device_step(): pl.pallas_call(functools.partial(step_kernel, num_dev, float(toks * num_d...]
    unnamed x19 -> x4, local copies, waits for them, and re-layouts: 3.77 us -> 6.56 us
    reshape x4 -> x0, local copies, waits for them, and re-layouts: 2.77 us -> none  [the longest x2 2.12 us: pack_parts(): part_a.reshape(3, num_dev, 5, 8, 8).transpose(1, 3, 2, 0, 4)]
    transpose x3 -> x0, local copies, waits for them, and re-layouts: 2.07 us -> none  [the longest x1 1.77 us: pack_parts(): part_a.reshape(3, num_dev, 5, 8, 8).transpose(1, 3, 2, 0, 4)]
    concatenate x1 -> x0, other arithmetic: 1.89 us -> none  [pack_parts(): return jnp.concatenate([main_b, rem_b, rows_a], axis=1)]
where the time goes in v2:
time: 56.7 us; the launch traced here: 56.4 us
  Pallas kernels  48.1 us (85%)
  local copies, waits for them, and re-layouts  7.7 us (14%)
  between operations  0.64 us (1%)
    pallas_call x1, Pallas kernels, device_step(): pl.pallas_call(functools.partial(step_kernel, num_dev, float(toks * num_d...  48.1 us
    unnamed x4, local copies, waits for them, and re-layouts  6.56 us
    squeeze x1, local copies, waits for them, and re-layouts, device_step(): return (alpha[0, :3], comb_a, comb_b)  1.14 us

profile of v2, /device:TPU:0, one launch (start us, length us, event | category | flops | bytes accessed | tf_op | source)
XLA Modules:
  0.0 56.4 jit_solution(6668892081403754465)
XLA Ops:
  0.6 1.6 %copy.10.a_hbm = bf16[1280,8]{1,0:T(8,128)(2,1)} copy(bf16[1280,8]{0,1:T(8,128)(2,1)} %param.11) | data formatting | bytes 40960 | tf_op args[4]
  2.3 2.2 %copy.11.heads_hbm = bf16[3,1280,13]{2,1,0:T(8,128)(2,1)} copy(bf16[3,1280,13]{1,2,0:T(8,128)(2,1)} %param.13) | data formatting | bytes 199680 | tf_op args[6]
  4.5 48.1 %grad_step.1 = (f32[1,128]{1,0:T(1,128)}, f32[40,8]{1,0:T(8,128)}, f32[8,160]{1,0:T(8,128)}) custom-call(bf16[256,1280]{1,0:T(8,128)(2,1)} %x_hbm.1, s32[3,256]{1,0:T(4,128)} %y_hbm.1, bf16[1280,5120]{1,0:T(8,128)(2,1)} %w1_hbm.1, bf16[5120,1280]{1,0:T(8,128)(2,1)} %w2_hbm.1, bf16[1280,8]{1,0:T(8,128)(2,1)} %copy.10.a_hbm, bf16[8,5120]{1,0:T(8,128)(2,1)} %bm_hbm.1, ...), custom_call_target="tpu_custom_call" | custom-call | tf_op jit(solution)/shard_map/grad_step/pallas_call | solution.py:337
  52.6 1.1 %slice_bitcast_fusion = f32[3]{0:T(128)} fusion(f32[1,128]{1,0:T(1,128)} %get-tuple-element.6), kind=kLoop, calls=%fused_computation | loop fusion | bytes 24 | tf_op jit(solution)/shard_map/squeeze | solution.py:386
  53.7 1.4 %copy.12 = f32[40,8]{0,1:T(8,128)} copy(f32[40,8]{1,0:T(8,128)} %get-tuple-element.10) | data formatting | bytes 2560
  55.1 1.3 %copy.14 = f32[8,160]{1,0:T(8,128)} copy(f32[8,160]{1,0:T(8,128)} %get-tuple-element.17) | data formatting | bytes 10240

commit v3 on v2

v3 whole, which is shorter than its diff:
```python
import functools

import jax
import jax.numpy as jnp
from jax import lax
from jax.experimental import pallas as pl
from jax.experimental.pallas import tpu as pltpu
from jax.sharding import PartitionSpec as P

EG_STEPS = 20
FWD_COLS = 512
BWD_COLS = 1280
NUM_TASKS = 3
PLANE = 8
GELU_SCALE = 0.7978845608028654
GELU_CUBE = 0.044715
MESH = pl.DeviceIdType.MESH


def full_sum(tile):
    return jnp.sum(jnp.sum(tile, axis=0, keepdims=True), axis=1, keepdims=True)


def local_gram(main, rem, rows):
    lane = lax.broadcasted_iota(jnp.int32, (8, 128), 1)
    rem_task = lane // 32
    row_task = (lane % 24) // 8
    rem_1, rem_2 = pltpu.roll(rem, 96, 1), pltpu.roll(rem, 64, 1)
    row_1, row_2 = pltpu.roll(rows, 120, 1), pltpu.roll(rows, 112, 1)

    def entry(t, s, rem_other, row_other):
        tile = main[t] * main[s]
        tile = tile + jnp.where(rem_task == t, rem * rem_other, 0.0)
        return full_sum(tile + jnp.where(row_task == t, rows * row_other, 0.0))

    entries = [entry(0, 0, rem, rows), entry(1, 1, rem, rows), entry(2, 2, rem, rows)]
    entries += [entry(0, 1, rem_1, row_1), entry(1, 2, rem_1, row_1), entry(0, 2, rem_2, row_2)]
    lane_row = lax.broadcasted_iota(jnp.int32, (1, 128), 1)
    gram_row = jnp.zeros((1, 128), jnp.float32)
    for k, value in enumerate(entries):
        gram_row = jnp.where(lane_row == k, value, gram_row)
    return gram_row


def solve_weights(gram_row):
    lane_row = lax.broadcasted_iota(jnp.int32, (1, 128), 1)
    m00, m11, m22, m01, m12, m02 = [jnp.sum(jnp.where(lane_row == k, gram_row, 0.0), axis=1, keepdims=True) for k in range(6)]
    to_exponent = 1.4426950408889634 / ((m00 + m11 + m22) / 3.0)
    m00, m11, m22, m01, m12, m02 = [m * to_exponent for m in (m00, m11, m22, m01, m12, m02)]

    g0 = g1 = g2 = jnp.zeros((1, 1), jnp.float32)
    for step in range(EG_STEPS + 1):
        e0, e1, e2 = jnp.exp2(-g0), jnp.exp2(-g1), jnp.exp2(-g2)
        inverse = 1.0 / (e0 + e1 + e2)
        if step < EG_STEPS:
            g0 = g0 + (m00 * e0 + m01 * e1 + m02 * e2) * inverse
            g1 = g1 + (m01 * e0 + m11 * e1 + m12 * e2) * inverse
            g2 = g2 + (m02 * e0 + m12 * e1 + m22 * e2) * inverse
    return e0 * inverse, e1 * inverse, e2 * inverse


def write_shares(weights, main, rem, rows, out_ref):
    w0, w1, w2 = weights
    lane = lax.broadcasted_iota(jnp.int32, (8, 128), 1)
    rem_task, row_task = lane // 32, (lane % 24) // 8
    out_ref[0] = jnp.where(lane == 0, w0, jnp.where(lane == 1, w1, w2))
    rows = rows * jnp.where(row_task == 0, w0, jnp.where(row_task == 1, w1, w2))
    rows = rows + pltpu.roll(rows, 120, 1) + pltpu.roll(rows, 112, 1)
    out_ref[1] = rows
    out_ref[2] = w0 * main[0] + w1 * main[1] + w2 * main[2]
    rem = rem * jnp.where(rem_task == 0, w0, jnp.where(rem_task == 1, w1, w2))
    out_ref[3] = rem + pltpu.roll(rem, 96, 1) + pltpu.roll(rem, 64, 1)


def finish_kernel(tiles_ref, alpha_ref, ga_ref, gb_ref):
    alpha_ref[...] = tiles_ref[0, 0:1, 0:3]
    rows = tiles_ref[1].T
    ga_ref[...] = jnp.concatenate([rows[24 * k : 24 * k + 8, :] for k in range(5)], axis=1)
    gb_ref[:, 0:128] = tiles_ref[2]
    gb_ref[:, 128:160] = tiles_ref[3, :, 0:32]


def dot_t(lhs, rhs):
    return lax.dot_general(lhs, rhs, (((1,), (1,)), ((), ())), preferred_element_type=jnp.float32)


def dot_n(lhs, rhs):
    return jnp.dot(lhs, rhs, preferred_element_type=jnp.float32)


def gelu_and_slope(pre_act):
    square = pre_act * pre_act
    tanh = jnp.tanh(GELU_SCALE * pre_act * (1.0 + GELU_CUBE * square))
    cdf = 0.5 + 0.5 * tanh
    bell = (0.5 * GELU_SCALE) * (1.0 - tanh * tanh) * (1.0 + (3.0 * GELU_CUBE) * square)
    return pre_act * cdf, cdf + pre_act * bell


def logit_errors(logits, labels, num_classes):
    by_class = logits.T
    errors = []
    for t in range(NUM_TASKS):
        rows = by_class[16 * t : 16 * t + 16, :]
        cls = lax.broadcasted_iota(jnp.int32, rows.shape, 0)
        rows = jnp.where(cls < num_classes, rows, -jnp.inf)
        expo = jnp.exp(rows - jnp.max(rows, axis=0, keepdims=True))
        probs = expo / jnp.sum(expo, axis=0, keepdims=True)
        errors.append(probs - jnp.where(cls == labels[t : t + 1, :], 1.0, 0.0))
    errors.append(jnp.zeros((128 - 16 * NUM_TASKS, logits.shape[0]), jnp.float32))
    return jnp.concatenate(errors, axis=0).T


def pack_share_columns(main_cols, dest):
    first = 160 * dest // 128
    shift = 160 * dest - 128 * first
    main, rem = [], []
    for cols in main_cols:
        left = cols[:, 128 * first : 128 * first + 128]
        right = cols[:, 128 * first + 128 : 128 * first + 256]
        lane = lax.broadcasted_iota(jnp.int32, left.shape, 1)
        if shift == 0:
            main.append(left)
            rem.append(right)
        else:
            left, right = pltpu.roll(left, 128 - shift, 1), pltpu.roll(right, 128 - shift, 1)
            main.append(jnp.where(lane < 128 - shift, left, right))
            rem.append(right)
    lane = lax.broadcasted_iota(jnp.int32, (8, 128), 1)
    tail = jnp.where(lane < 32, rem[0], 0.0)
    tail = jnp.where(lane // 32 == 1, pltpu.roll(rem[1], 32, 1), tail)
    tail = jnp.where(lane // 32 == 2, pltpu.roll(rem[2], 64, 1), tail)
    return main, tail


def step_kernel(
    n, tok_total, num_classes,
    x_hbm, y_hbm, w1_hbm, w2_hbm, at_hbm, bm_hbm, ht_hbm,
    out_ref,
    x, y, w1, w2, at, bm, ht, slope, pre, z_acc, x_t, u_diag, bm_rep, hcat, err, dz, dp, du_acc,
    send_b, recv_b, sum_b, recv_z, send_a, recv_a, gram_send, gram_recv,
    in_sem, w1_sem, w2_sem, bsend_sem, brecv_sem, zsend_sem, zrecv_sem, asend_sem, arecv_sem, gsend_sem, grecv_sem,
):
    bf16, f32 = jnp.bfloat16, jnp.float32
    me = lax.axis_index("data")
    plane, spot = me // PLANE, me % PLANE
    planes = n // PLANE
    d_model, d_ff = w1_hbm.shape
    toks = x_hbm.shape[0]
    fwd_steps = d_ff // FWD_COLS

    small = [
        pltpu.make_async_copy(src, dst, in_sem.at[k])
        for k, (src, dst) in enumerate([(x_hbm, x), (at_hbm, at), (bm_hbm, bm), (ht_hbm, ht), (y_hbm, y)])
    ]
    def span(j):
        return pl.ds(pl.multiple_of(j * FWD_COLS, FWD_COLS), FWD_COLS)

    def w1_copy(j):
        return pltpu.make_async_copy(w1_hbm.at[:, span(j)], w1.at[:, span(j)], w1_sem.at[j])

    def w2_copy(j):
        return pltpu.make_async_copy(w2_hbm.at[span(j), :], w2.at[span(j), :], w2_sem.at[j])

    for copy in small:
        copy.start()
    w1_copy(0).start()

    def fetch(j, carry):
        w1_copy(j).start()
        w2_copy(j - 1).start()
        return carry

    lax.fori_loop(1, fwd_steps, fetch, 0)
    w2_copy(fwd_steps - 1).start()

    barrier = pltpu.get_barrier_semaphore()

    def greet(k, carry):
        pl.semaphore_signal(barrier, inc=1, device_id=(lax.rem(me + k, n),), device_id_type=MESH)
        return carry

    lax.fori_loop(1, n, greet, 0)

    for copy in small:
        copy.wait()
    low_rank = dot_t(x[...], at[...]).astype(bf16)

    def up_project(j):
        return dot_n(x[...], w1[:, span(j)]) + dot_n(low_rank, bm[:, span(j)])

    def activate(j):
        act, slope_tile = gelu_and_slope(pre[...])
        slope[:, span(j)] = slope_tile
        return act.astype(bf16)

    u_t = dot_t(at[...], x[...])
    blank = jnp.zeros_like(u_t)
    u_diag[...] = jnp.concatenate(
        [jnp.concatenate([u_t if s == t else blank for s in range(NUM_TASKS)], axis=1) for t in range(NUM_TASKS)], axis=0
    ).astype(bf16)
    bm_rep[...] = jnp.concatenate([bm[...].astype(f32)] * 16, axis=0).astype(bf16)
    gap = jnp.zeros((16 - num_classes, d_model), f32)
    heads = [part for t in range(NUM_TASKS) for part in (ht[t].astype(f32), gap)]
    hcat[...] = jnp.concatenate(heads + [jnp.zeros((128 - 16 * NUM_TASKS, d_model), f32)], axis=0).astype(bf16)
    x_t[...] = x[...].astype(f32).T.astype(bf16)

    z_acc[...] = jnp.zeros_like(z_acc)
    w1_copy(0).wait()
    pre[...] = up_project(0)

    def forward(j, carry):
        w1_copy(j + 1).wait()
        w2_copy(j).wait()
        act = activate(j)
        pre[...] = up_project(j + 1)
        z_acc[...] += dot_n(act, w2[span(j), :])
        return carry

    lax.fori_loop(0, fwd_steps - 1, forward, 0)
    w2_copy(fwd_steps - 1).wait()
    z_acc[...] += dot_n(activate(fwd_steps - 1), w2[span(fwd_steps - 1), :])

    trunk = (x[...].astype(f32) + z_acc[...]).astype(bf16)
    errors = logit_errors(dot_t(trunk, hcat[...]), y[...], num_classes)
    lane = lax.broadcasted_iota(jnp.int32, (toks, 128), 1)
    for t in range(NUM_TASKS):
        err[pl.ds(t * toks, toks), :] = jnp.where(lane // 16 == t, errors, 0.0).astype(bf16)
    dz[...] = dot_n(err[...], hcat[...]).astype(bf16)
    pl.semaphore_wait(barrier, n - 1)
    SEND_ON = True

    def plane_send(i):
        if not SEND_ON:
            return

        def send(k, carry):
            to = lax.rem(spot + k, PLANE)
            pltpu.make_async_remote_copy(
                src_ref=send_b.at[i, to], dst_ref=recv_b.at[i, spot], send_sem=bsend_sem, recv_sem=brecv_sem.at[i],
                device_id=(plane * PLANE + to,), device_id_type=MESH,
            ).start()
            return carry

        lax.fori_loop(1, PLANE, send, 0)
        recv_b[i, spot] = send_b[i, spot]

    def plane_wait(i):
        pltpu.make_async_remote_copy(
            src_ref=send_b.at[i, pl.ds(0, PLANE - 1)], dst_ref=recv_b.at[i, pl.ds(0, PLANE - 1)], send_sem=bsend_sem, recv_sem=brecv_sem.at[i],
            device_id=(lax.rem(me + 1, n),), device_id_type=MESH,
        ).wait_recv()

    def across_send(i):
        if not SEND_ON:
            return
        plane_wait(i)
        sum_b[i] = jnp.sum(recv_b[i], axis=0)
        pltpu.make_async_remote_copy(
            src_ref=sum_b.at[i], dst_ref=recv_z.at[i], send_sem=zsend_sem, recv_sem=zrecv_sem,
            device_id=(lax.rem(plane + 1 + i, planes) * PLANE + spot,), device_id_type=MESH,
        ).start()

    def chunk_cols(i):
        chunk = lax.rem(plane + 1 + i, planes)
        return pl.ds(pl.multiple_of(chunk * BWD_COLS, BWD_COLS), BWD_COLS)

    def back_project(i):
        cols = chunk_cols(i)
        d_hidden = dot_t(dz[...], w2[cols, :])
        slope_tile = slope[:, cols]
        for t in range(NUM_TASKS):
            dp[pl.ds(t * toks, toks), :] = (d_hidden[t * toks : (t + 1) * toks, :] * slope_tile).astype(bf16)

    def low_rank_grad(i):
        du_acc[...] += dot_t(dp[...], bm_rep[:, chunk_cols(i)])

    def adapter_grad(i):
        grads = dot_n(u_diag[...], dp[...])
        for to in range(PLANE):
            main, tail = pack_share_columns([grads[8 * t : 8 * t + 8, :] for t in range(NUM_TASKS)], to)
            for t in range(NUM_TASKS):
                send_b[i, to, t] = main[t]
            send_b[i, to, NUM_TASKS] = tail

    du_acc[...] = jnp.zeros_like(du_acc)

    def backward(i, carry):
        back_project(i)
        low_rank_grad(i)
        adapter_grad(i)
        plane_send(i)

        @pl.when(i >= 1)
        def _():
            across_send(i - 1)

        return carry

    lax.fori_loop(0, planes, backward, 0)

    lane = lax.broadcasted_iota(jnp.int32, (toks, 128), 1)
    du = du_acc[2 * toks :, :]
    for t in range(NUM_TASKS - 1):
        du = jnp.where((lane // 8) % NUM_TASKS == t, du_acc[t * toks : (t + 1) * toks, :], du)
    rows_a = dot_n(x_t[...], du.astype(bf16)).reshape(n, 5, 8, 128)
    lane = lax.broadcasted_iota(jnp.int32, (n, 8, 128), 2)
    packed = jnp.where(lane < 120, rows_a[:, 4], 0.0)
    for k in range(4):
        packed = jnp.where(lane // 24 == k, rows_a[:, k], packed)
    send_a[...] = packed

    def send_rows(k, carry):
        to = lax.rem(me + k, n)
        pltpu.make_async_remote_copy(
            src_ref=send_a.at[to], dst_ref=recv_a.at[me], send_sem=asend_sem, recv_sem=arecv_sem,
            device_id=(to,), device_id_type=MESH,
        ).start()
        return carry

    lax.fori_loop(PLANE, n, send_rows, 0)
    lax.fori_loop(1, PLANE, send_rows, 0)
    recv_a[me] = send_a[me]

    plane_wait(planes - 1)
    every_z = pltpu.make_async_remote_copy(
        src_ref=sum_b, dst_ref=recv_z, send_sem=zsend_sem, recv_sem=zrecv_sem, device_id=(lax.rem(me + 1, n),), device_id_type=MESH
    )
    every_z.wait_recv()
    share_b = (jnp.sum(recv_b[planes - 1], axis=0) + jnp.sum(recv_z[...], axis=0)) / tok_total
    main, rem = (share_b[0], share_b[1], share_b[2]), share_b[3]
    every_a = pltpu.make_async_remote_copy(
        src_ref=send_a.at[pl.ds(0, n - 1)], dst_ref=recv_a.at[pl.ds(0, n - 1)], send_sem=asend_sem, recv_sem=arecv_sem,
        device_id=(lax.rem(me + 1, n),), device_id_type=MESH,
    )
    every_a.wait_recv()
    rows = jnp.sum(recv_a[...], axis=0) / tok_total
    gram_row = local_gram(main, rem, rows)
    gram_send[...] = gram_row
    gram_recv[me] = gram_row

    def send_gram(k, carry):
        pltpu.make_async_remote_copy(
            src_ref=gram_send, dst_ref=gram_recv.at[me], send_sem=gsend_sem, recv_sem=grecv_sem,
            device_id=(lax.rem(me + k, n),), device_id_type=MESH,
        ).start()
        return carry

    lax.fori_loop(PLANE, n, send_gram, 0)
    lax.fori_loop(1, PLANE, send_gram, 0)
    every_gram = pltpu.make_async_remote_copy(
        src_ref=gram_recv.at[pl.ds(0, n - 1)], dst_ref=gram_recv.at[pl.ds(0, n - 1)], send_sem=gsend_sem, recv_sem=grecv_sem,
        device_id=(lax.rem(me + 1, n),), device_id_type=MESH,
    )
    pltpu.make_async_remote_copy(
        src_ref=send_b.at[:, pl.ds(0, PLANE - 1)], dst_ref=recv_b.at[:, pl.ds(0, PLANE - 1)], send_sem=bsend_sem, recv_sem=brecv_sem.at[0],
        device_id=(lax.rem(me + 1, n),), device_id_type=MESH,
    ).wait_send()
    every_z.wait_send()
    every_a.wait_send()
    every_gram.wait_recv()
    weights = solve_weights(jnp.sum(gram_recv[...], axis=0))
    write_shares(weights, main, rem, rows, out_ref)
    every_gram.wait_send()


def solution(mesh):
    num_dev = mesh.shape["data"]

    def device_step(tokens, labels, w_one, w_two, adapter_a, adapter_b, task_heads):
        toks, d_model = tokens.shape
        d_ff = w_one.shape[1]
        planes = num_dev // PLANE
        fwd_steps = d_ff // FWD_COLS
        bf16, f32 = jnp.bfloat16, jnp.float32
        dma = pltpu.SemaphoreType.DMA
        vmem = pl.BlockSpec(memory_space=pltpu.VMEM)
        hbm = pl.BlockSpec(memory_space=pltpu.HBM)
        adapter_t = adapter_a.T
        heads_t = task_heads.transpose(0, 2, 1)
        tiles = pl.pallas_call(
            functools.partial(step_kernel, num_dev, float(toks * num_dev), task_heads.shape[2]),
            out_shape=jax.ShapeDtypeStruct((4, 8, 128), f32),
            in_specs=[hbm] * 7,
            out_specs=vmem,
            scratch_shapes=[
                pltpu.VMEM(tokens.shape, bf16),
                pltpu.VMEM(labels.shape, jnp.int32),
                pltpu.VMEM(w_one.shape, bf16),
                pltpu.VMEM(w_two.shape, bf16),
                pltpu.VMEM(adapter_t.shape, bf16),
                pltpu.VMEM(adapter_b.shape, bf16),
                pltpu.VMEM(heads_t.shape, bf16),
                pltpu.VMEM((toks, d_ff), f32),
                pltpu.VMEM((toks, FWD_COLS), f32),
                pltpu.VMEM((toks, d_model), f32),
                pltpu.VMEM((d_model, toks), bf16),
                pltpu.VMEM((8 * NUM_TASKS, NUM_TASKS * toks), bf16),
                pltpu.VMEM((128, d_ff), bf16),
                pltpu.VMEM((128, d_model), bf16),
                pltpu.VMEM((NUM_TASKS * toks, 128), bf16),
                pltpu.VMEM((NUM_TASKS * toks, d_model), bf16),
                pltpu.VMEM((NUM_TASKS * toks, BWD_COLS), bf16),
                pltpu.VMEM((NUM_TASKS * toks, 128), f32),
                pltpu.VMEM((planes, PLANE, 4, 8, 128), f32),
                pltpu.VMEM((planes, PLANE, 4, 8, 128), f32),
                pltpu.VMEM((planes - 1, 4, 8, 128), f32),
                pltpu.VMEM((planes - 1, 4, 8, 128), f32),
                pltpu.VMEM((num_dev, 8, 128), f32),
                pltpu.VMEM((num_dev, 8, 128), f32),
                pltpu.VMEM((1, 128), f32),
                pltpu.VMEM((num_dev, 1, 128), f32),
                dma((5,)),
                dma((fwd_steps,)),
                dma((fwd_steps,)),
                dma,
                dma((planes,)),
                dma,
                dma,
                dma,
                dma,
                dma,
                dma,
            ],
            compiler_params=pltpu.CompilerParams(collective_id=0, has_side_effects=True, vmem_limit_bytes=60 * 1024 * 1024),
            name="grad_step",
        )(tokens, labels, w_one, w_two, adapter_t, adapter_b, heads_t)
        alpha, comb_at, comb_b = pl.pallas_call(
            finish_kernel,
            out_shape=(
                jax.ShapeDtypeStruct((1, NUM_TASKS), f32),
                jax.ShapeDtypeStruct((8, d_model // num_dev), f32),
                jax.ShapeDtypeStruct((8, d_ff // num_dev), f32),
            ),
            in_specs=[vmem],
            out_specs=(vmem, vmem, vmem),
            name="write_out",
        )(tiles)
        return alpha[0], comb_at.T, comb_b

    return jax.shard_map(device_step, mesh=mesh, in_specs=(P("data", None), P(None, "data"), P(), P(), P(), P(), P()), out_specs=(P(), P("data", None), P(None, "data")), check_vma=False)
```

time: 56.7 us -> 46.3 us (0.82)
  local copies, waits for them, and re-layouts: 7.7 us -> 0 us
  Pallas kernels: 48.1 us -> 45.5 us
    unnamed x4 -> x0, local copies, waits for them, and re-layouts: 6.56 us -> none
    pallas_call x1, Pallas kernels: 48.1 us -> 44 us  [device_step(): pl.pallas_call(functools.partial(step_kernel, num_dev, float(toks * num_d...]
    pallas_call x0 -> x1, Pallas kernels: none -> 1.48 us  [device_step(): pl.pallas_call(finish_kernel, out_shape=(jax.ShapeDtypeStruct((1, NUM_TAS...]
    squeeze x1 -> x0, local copies, waits for them, and re-layouts: 1.14 us -> none  [device_step(): return (alpha[0, :3], comb_a, comb_b)]
where the time goes in v3:
time: 46.3 us; the launch traced here: 46.1 us
  Pallas kernels  45.5 us (98%)
  between operations  0.64 us (1%)
    pallas_call x1, Pallas kernels, device_step(): pl.pallas_call(functools.partial(step_kernel, num_dev, float(toks * num_d...  44 us
    pallas_call x1, Pallas kernels, device_step(): pl.pallas_call(finish_kernel, out_shape=(jax.ShapeDtypeStruct((1, NUM_TAS...  1.48 us

profile of v3, /device:TPU:0, one launch (start us, length us, event | category | flops | bytes accessed | tf_op | source)
XLA Modules:
  0.0 46.1 jit_solution(8717042038181120619)
XLA Ops:
  0.6 44.0 %grad_step.1.tiles_ref = f32[4,8,128]{2,1,0:T(8,128)} custom-call(bf16[256,1280]{1,0:T(8,128)(2,1)} %x_hbm.1, s32[3,256]{1,0:T(4,128)} %y_hbm.1, bf16[1280,5120]{1,0:T(8,128)(2,1)} %w1_hbm.1, bf16[5120,1280]{1,0:T(8,128)(2,1)} %w2_hbm.1, bf16[8,1280]{1,0:T(8,128)(2,1)} %bitcast.5, bf16[8,5120]{1,0:T(8,128)(2,1)} %bm_hbm.1, bf16[3,13,1280]{2,1,0:T(8,128)(2,1)} %bitcast.4), custom_call_target="tpu_custom_call" | custom-call | tf_op jit(solution)/shard_map/grad_step/pallas_call | solution.py:380
  44.6 1.5 %write_out.1 = (f32[1,3]{1,0:T(1,128)}, f32[8,40]{1,0:T(8,128)}, f32[8,160]{1,0:T(8,128)}) custom-call(f32[4,8,128]{2,1,0:T(8,128)} %grad_step.1.tiles_ref), custom_call_target="tpu_custom_call" | custom-call | tf_op jit(solution)/shard_map/write_out/pallas_call | solution.py:427

commit v4 on v3

--- a/solution.py
+++ b/solution.py
@@ -421,9 +421,9 @@
                 dma,
                 dma,
             ],
-            compiler_params=pltpu.CompilerParams(collective_id=0, has_side_effects=True, vmem_limit_bytes=60 * 1024 * 1024),
+            compiler_params=pltpu.CompilerParams(collective_id=0, has_side_effects=True, vmem_limit_bytes=52 * 1024 * 1024),
             name="grad_step",
-        )(tokens, labels, w_one, w_two, adapter_t, adapter_b, heads_t)
+        )(*[pltpu.with_memory_space_constraint(arg, pltpu.HBM) for arg in (tokens, labels, w_one, w_two, adapter_t, adapter_b, heads_t)])
         alpha, comb_at, comb_b = pl.pallas_call(
             finish_kernel,
             out_shape=(
@@ -433,6 +433,7 @@
             ),
             in_specs=[vmem],
             out_specs=(vmem, vmem, vmem),
+            compiler_params=pltpu.CompilerParams(vmem_limit_bytes=1024 * 1024),
             name="write_out",
         )(tiles)
         return alpha[0], comb_at.T, comb_b

time: 46.3 us -> 44.9 us (0.970)
  Pallas kernels: 45.5 us -> 44.2 us
    pallas_call x1, Pallas kernels: 1.48 us -> 0.77 us  [device_step(): pl.pallas_call(finish_kernel, out_shape=(jax.ShapeDtypeStruct((1, NUM_TAS...]
    pallas_call x1, Pallas kernels: 44 us -> 43.4 us  [device_step(): pl.pallas_call(functools.partial(step_kernel, num_dev, float(toks * num_d...]
where the time goes in v4:
time: 44.9 us; the launch traced here: 44.8 us
  Pallas kernels  44.2 us (98%)
  between operations  0.64 us (1%)
    pallas_call x1, Pallas kernels, device_step(): pl.pallas_call(functools.partial(step_kernel, num_dev, float(toks * num_d...  43.4 us

profile of v4, /device:TPU:0, one launch (start us, length us, event | category | flops | bytes accessed | tf_op | source)
XLA Modules:
  0.0 44.8 jit_solution(8511181411903783311)
XLA Ops:
  0.6 43.4 %grad_step.1.tiles_ref = f32[4,8,128]{2,1,0:T(8,128)S(1)} custom-call(bf16[256,1280]{1,0:T(8,128)(2,1)} %x_hbm.1, s32[3,256]{1,0:T(4,128)} %y_hbm.1, bf16[1280,5120]{1,0:T(8,128)(2,1)} %w1_hbm.1, bf16[5120,1280]{1,0:T(8,128)(2,1)} %w2_hbm.1, bf16[8,1280]{1,0:T(8,128)(2,1)} %bitcast.5, bf16[8,5120]{1,0:T(8,128)(2,1)} %bm_hbm.1, bf16[3,13,1280]{2,1,0:T(8,128)(2,1)} %bitcast.4), custom_call_target="tpu_custom_call" | custom-call | tf_op jit(solution)/shard_map/grad_step/pallas_call | solution.py:380
  44.0 0.8 %write_out.1 = (f32[1,3]{1,0:T(1,128)}, f32[8,40]{1,0:T(8,128)}, f32[8,160]{1,0:T(8,128)}) custom-call(f32[4,8,128]{2,1,0:T(8,128)S(1)} %grad_step.1.tiles_ref), custom_call_target="tpu_custom_call" | custom-call | tf_op jit(solution)/shard_map/write_out/pallas_call | solution.py:427
